TPU v7x, 32 devices: a whole 2x2x4 slice. The times are simulated.
32 devices in a mesh: groups: 2 (over y), fsdp: 4 (over z), tensor: 4 (over x, core).
Axes of the slice: x: 2, y: 2, z: 4, core: 2. Of those that a mesh axis runs over, the one named last changes fastest.
Arguments:
- tokens: bfloat16 [2048, 4608], P(('groups', 'fsdp'), 'tensor'), parts along dimension 0, may hold values from -100 to 100
- norm_gain: bfloat16 [4608], P('tensor'), may hold values from 0.25 to 1.75
- w_query: bfloat16 [4608, 4096], P('fsdp', 'tensor'), may hold values from -0.5 to 0.5
- w_key: bfloat16 [4608, 2048], P('fsdp', 'tensor'), may hold values from -0.09375 to 0.09375
- w_value: bfloat16 [4608, 2048], P('fsdp', 'tensor'), may hold values from -0.09375 to 0.09375
- w_out: bfloat16 [4096, 4608], P('tensor', 'fsdp'), may hold values from -0.5 to 0.5
- post_gain: bfloat16 [4608], P('tensor'), may hold values from 0.25 to 1.75
Outputs:
- mixed: float32 [2048, 4608], P(('groups', 'fsdp'), 'tensor'), parts along dimension 0
There are 2 independent parts, one for each index of `groups`. A program takes and returns all parts, laid end to end along the dimension named above; an argument that names none is the same for every part. Nothing has to cross between parts.
All inputs are finite; a program needn't handle non-finite values.
Results may differ from a plain program's by a relative error of at most 0.0053.
Values may be sent and summed in bfloat16 or wider, within the bound.
A program may use at most 128 MiB of HBM per device.

v0:
```python
import jax
import jax.numpy as jnp
from jax import lax
from jax.sharding import PartitionSpec as P

D = 4608
HEAD_DIM = 128


eps_norm = 1e-06
soft_cap = 50.0
attn_scale = 144.0 ** (-0.5)
rope_base = 10000.0


def rotate(values, position):
    head_dim = values.shape[-1]
    half = head_dim // 2
    freq = rope_base ** (-(jnp.arange(half, dtype=jnp.float32) * 2.0 / head_dim))
    angle = position.astype(jnp.float32)[:, None] * freq[None, :]
    cosine = jnp.cos(angle)[:, None, :]
    sine = jnp.sin(angle)[:, None, :]
    first = values[..., :half]
    second = values[..., half:]
    return jnp.concatenate(
        [first * cosine - second * sine, second * cosine + first * sine], axis=-1
    )


def attend(query, keys, values, position):
    count, heads, head_dim = query.shape
    kv_count = keys.shape[1]
    grouped = query.reshape(count, kv_count, heads // kv_count, head_dim)
    scores = (
        jnp.einsum("nkgd,mkd->kgnm", grouped, keys, preferred_element_type=jnp.float32) * attn_scale
    )
    capped = soft_cap * jnp.tanh(scores / soft_cap)
    allowed = position[None, :] <= position[:, None]
    weights = jnp.where(allowed, jnp.exp(capped), 0.0)
    probs = (weights / jnp.sum(weights, axis=-1, keepdims=True)).astype(jnp.bfloat16)
    mixed = jnp.einsum("kgnm,mkd->nkgd", probs, values, preferred_element_type=jnp.float32)
    return mixed.reshape(count, heads * head_dim).astype(jnp.bfloat16)


def on_device(tokens, norm_gain, w_query, w_key, w_value, w_out, post_gain):
    rows = tokens.shape[0]
    full_tokens, full_gain = (
        lax.all_gather(tokens, "tensor", axis=1, tiled=True),
        lax.all_gather(norm_gain, "tensor", axis=0, tiled=True),
    )
    widened = full_tokens.astype(jnp.float32)
    total = jnp.sum(widened * widened, axis=1)
    whole = (
        widened * lax.rsqrt(total / D + eps_norm)[:, None] * full_gain.astype(jnp.float32)
    ).astype(jnp.bfloat16)
    pieces = (
        lax.all_gather(w_query, "fsdp", axis=0, tiled=True),
        lax.all_gather(w_key, "fsdp", axis=0, tiled=True),
        lax.all_gather(w_value, "fsdp", axis=0, tiled=True),
    )
    query_raw, key_raw, value_raw = tuple(
        (jnp.dot(whole, piece, preferred_element_type=jnp.float32) for piece in pieces)
    )
    position = jnp.arange(rows, dtype=jnp.int32)
    local_heads = w_query.shape[1] // HEAD_DIM
    local_kv = w_key.shape[1] // HEAD_DIM
    query = rotate(query_raw.reshape(rows, local_heads, HEAD_DIM), position).astype(jnp.bfloat16)
    key = rotate(key_raw.reshape(rows, local_kv, HEAD_DIM), position).astype(jnp.bfloat16)
    value = value_raw.astype(jnp.bfloat16).reshape(rows, local_kv, HEAD_DIM)
    attn = attend(query, key, value, position)
    partial_value = jnp.dot(
        attn, lax.all_gather(w_out, "fsdp", axis=1, tiled=True), preferred_element_type=jnp.float32
    )
    proj = lax.psum_scatter(
        partial_value.astype(jnp.bfloat16), "tensor", scatter_dimension=1, tiled=True
    ).astype(jnp.float32)
    post_total = lax.psum(jnp.sum(proj * proj, axis=1), "tensor")
    branch = proj * lax.rsqrt(post_total / D + eps_norm)[:, None] * post_gain.astype(jnp.float32)
    return tokens.astype(jnp.float32) + branch


def solution(mesh):
    placed = (
        P(("groups", "fsdp"), "tensor"),
        P("tensor"),
        P("fsdp", "tensor"),
        P("fsdp", "tensor"),
        P("fsdp", "tensor"),
        P("tensor", "fsdp"),
        P("tensor"),
    )
    return jax.shard_map(
        on_device,
        mesh=mesh,
        in_specs=placed,
        out_specs=P(("groups", "fsdp"), "tensor"),
        check_vma=False,
    )
```

profile of v0, /device:TPU:0, one launch (start us, length us, event | category | flops | bytes accessed | tf_op | source)
XLA Modules:
  0.0 604.8 jit_solution(8890563282905837423)
XLA Ops:
  6.5 0.0 all-gather.7.cloned.1.call-start
  6.5 0.7 all-gather.7.cloned.1.call-update
  7.3 0.0 all-gather.9.cloned.1.call-start
  7.3 0.7 all-gather.9.cloned.1.call-update
  8.0 0.0 all-gather.11.cloned.1.call-start
  8.1 0.7 all-gather.11.cloned.1.call-update
  8.7 0.0 copy-start.3
  8.8 0.0 all-gather.13.cloned.1.call-start
  8.8 0.5 all-gather.13.cloned.1.call-update
  9.3 0.0 all-gather.15.cloned.1.call-start
  9.4 0.5 all-gather.15.cloned.1.call-update
  9.9 0.0 reduce-scatter.4.cloned.1.call-start
  10.0 0.0 copy-done.3
  10.0 6.2 %all-gather = bf16[4,1,1152]{2,1,0:T(2,128)(2,1)S(1)} all-gather(bf16[1,1,1152]{2,1,0:T(2,128)(2,1)S(1)} %reshape.85), channel_id=1, replica_groups=mesh['groups'=2,'fsdp'=4,'tensor'=4] {'tensor'}, dimensions={0}, use_global_device_ids=true | all-gather | bytes 11520 | tf_op jit(solution)/shard_map/all_gather | solution.py:49
  16.2 0.1 convert_reduce_fusion
  16.4 0.5 multiply_cosine_fusion
  16.9 18.8 %all-gather.7.cloned.1.call-done = bf16[256,4608]{1,0:T(8,128)(2,1)} async-done(((bf16[256,1152]{1,0:T(8,128)(2,1)}), bf16[256,4608]{1,0:T(8,128)(2,1)}) %all-gather.7.cloned.1.call-update) | async-done | bytes 2359312 | tf_op jit(solution)/shard_map/all_gather | solution.py:48
  35.7 0.0 copy-start
  35.7 2.4 fusion
  38.1 88.6 %all-gather.9.cloned.1.call-done = bf16[4608,512]{1,0:T(8,128)(2,1)} async-done(((bf16[1152,512]{1,0:T(8,128)(2,1)}), bf16[4608,512]{1,0:T(8,128)(2,1)}) %all-gather.9.cloned.1.call-update) | async-done | bytes 4718608 | tf_op jit(solution)/shard_map/all_gather | solution.py:59
  126.7 0.0 copy-done
  126.7 3.8 convolution_convert_fusion.2
  130.5 0.1 copy.23
  130.6 85.4 %all-gather.11.cloned.1.call-done = bf16[4608,512]{1,0:T(8,128)(2,1)} async-done(((bf16[1152,512]{1,0:T(8,128)(2,1)}), bf16[4608,512]{1,0:T(8,128)(2,1)}) %all-gather.11.cloned.1.call-update) | async-done | bytes 4718608 | tf_op jit(solution)/shard_map/all_gather | solution.py:58
  216.1 4.6 fusion.15
  220.7 1.2 reshape.83
  221.9 0.3 fusion.18
  222.2 0.1 subtract_convert_fusion.1
  222.4 160.3 %all-gather.13.cloned.1.call-done = bf16[4608,1024]{1,0:T(8,128)(2,1)} async-done(((bf16[1152,1024]{1,0:T(8,128)(2,1)}), bf16[4608,1024]{1,0:T(8,128)(2,1)}) %all-gather.13.cloned.1.call-update) | async-done | bytes 9437200 | tf_op jit(solution)/shard_map/all_gather | solution.py:57
  382.7 5.3 convolution_bitcast_fusion
  388.0 0.2 copy.28
  388.2 0.5 subtract_convert_fusion
  388.7 0.1 copy.17
  388.8 0.1 copy.16
  388.9 2.3 bitcast_select_fusion
  391.2 3.2 convolution_convert_fusion.1
  394.4 154.7 %all-gather.15.cloned.1.call-done = bf16[1024,4608]{1,0:T(8,128)(2,1)} async-done(((bf16[1024,1152]{1,0:T(8,128)(2,1)}), bf16[1024,4608]{1,0:T(8,128)(2,1)}) %all-gather.15.cloned.1.call-update) | async-done | bytes 9437200 | tf_op jit(solution)/shard_map/all_gather | solution.py:72
  549.1 6.6 %convolution_convert_fusion = bf16[256,4608]{1,0:T(8,128)(2,1)S(1)} fusion(bf16[256,1024]{0,1:T(8,128)(2,1)S(1)} %bitcast.31, bf16[1024,4608]{1,0:T(8,128)(2,1)} %all-gather.15.cloned.1.call-done), kind=kOutput, calls=%fused_computation | convolution fusion | flops 2417098752 | bytes 12320768 | tf_op jit(solution)/shard_map/dot_general | solution.py:71
  555.7 2.4 copy.24
  558.1 0.0 copy-start.2
  558.2 0.0 reduce-scatter.4.cloned.1.call-update
  558.2 0.7 copy-done.2
  558.8 30.5 %reduce-scatter.4.cloned.1.call-done = bf16[1152,256]{1,0:T(8,128)(2,1)} async-done(((bf16[4608,256]{1,0:T(8,128)(2,1)}), bf16[1152,256]{1,0:T(8,128)(2,1)}) %reduce-scatter.4.cloned.1.call-update) | async-done | bytes 589840
  589.4 1.4 copy.25
  590.7 0.2 fusion.3
  590.9 5.8 psum.7
  596.7 0.0 copy-done.1
  596.7 1.3 fusion.5
  (9 shorter events, 0.1 us)
Async XLA Ops:
  6.5 29.2 %all-gather.7.cloned.1.call-start = ((), (), s32[]{:S(2)}) async-start(), calls=%async_computation.1 | async-start | bytes 2949120 | tf_op jit(solution)/shard_map/all_gather | solution.py:48
  7.3 119.4 %all-gather.9.cloned.1.call-start = ((), (), s32[]{:S(2)}) async-start(), calls=%async_computation.2 | async-start | bytes 5898240 | tf_op jit(solution)/shard_map/all_gather | solution.py:59
  8.0 208.1 %all-gather.11.cloned.1.call-start = ((), (), s32[]{:S(2)}) async-start(), calls=%async_computation.3 | async-start | bytes 5898240 | tf_op jit(solution)/shard_map/all_gather | solution.py:58
  8.7 1.2 copy-start.3
  8.8 374.0 %all-gather.13.cloned.1.call-start = ((), (), s32[]{:S(2)}) async-start(), calls=%async_computation.4 | async-start | bytes 11796480 | tf_op jit(solution)/shard_map/all_gather | solution.py:57
  9.3 539.8 %all-gather.15.cloned.1.call-start = ((), (), s32[]{:S(2)}) async-start(), calls=%async_computation.5 | async-start | bytes 11796480 | tf_op jit(solution)/shard_map/all_gather | solution.py:72
  9.9 579.4 %reduce-scatter.4.cloned.1.call-start = ((), (), s32[]{:S(2)}) async-start(), calls=%async_computation.6 | async-start | bytes 2949120
  35.7 91.0 %copy-start = (bf16[256,4608]{1,0:T(8,128)(2,1)S(1)}, bf16[256,4608]{1,0:T(8,128)(2,1)}, u32[]{:S(2)}) copy-start(bf16[256,4608]{1,0:T(8,128)(2,1)} %all-gather.7.cloned.1.call-done) | copy-start | bytes 7077892
  558.1 0.7 copy-start.2
  558.2 38.5 %copy-start.1 = (bf16[256,1152]{1,0:T(8,128)(2,1)S(1)}, bf16[256,1152]{1,0:T(8,128)(2,1)}, u32[]{:S(2)}) copy-start(bf16[256,1152]{1,0:T(8,128)(2,1)} %param.7) | copy-start | bytes 1769476
Sparse Core Ops, SparseCore 0:
  8.9 26.7 all-gather.6
  37.3 89.3 all-gather.8
  128.2 87.7 all-gather.10
  217.5 165.1 all-gather.12
  384.1 164.9 all-gather.14
  558.3 31.0 reduce-scatter.3
where the time goes:
time: 605 us
  waiting for transfers between devices  542 us (90%)
  matrix products  25.8 us (4%)
  between operations  13.6 us (2%)
  blocking collectives  12 us (2%)
  local copies, waits for them, and re-layouts  6.52 us (1%)
    all_gather x1, waiting for transfers between devices, on_device(): lax.all_gather(w_query, 'fsdp', axis=0, tiled=True)  160 us
    all_gather x1, waiting for transfers between devices, on_device(): lax.all_gather(w_out, 'fsdp', axis=1, tiled=True)  155 us
    all_gather x1, waiting for transfers between devices, on_device(): lax.all_gather(w_value, 'fsdp', axis=0, tiled=True)  88.6 us
    all_gather x1, waiting for transfers between devices, on_device(): lax.all_gather(w_key, 'fsdp', axis=0, tiled=True)  85.4 us
    unnamed x7, waiting for transfers between devices  33.7 us
    all_gather x1, waiting for transfers between devices, on_device(): lax.all_gather(tokens, 'tensor', axis=1, tiled=True)  18.8 us
    dot_general x3, matrix products, on_device(): jnp.dot(whole, piece, preferred_element_type=jnp.float32)  13.7 us
  transfers between devices with their start and end apart: 6, of which 6 were waited for; matrix products, arithmetic and copies ran while one was open for 4% of the time, Pallas kernels for 0%

commit v1 on v0

v1 whole, which is shorter than its diff:
```python
import jax
import jax.numpy as jnp
from jax import lax
from jax.sharding import PartitionSpec as P

HEAD_DIM = 128

eps_norm = 1e-06
soft_cap = 50.0
attn_scale = 144.0 ** (-0.5)
rope_base = 10000.0


def rotate(values, position):
    head_dim = values.shape[-1]
    half = head_dim // 2
    freq = rope_base ** (-(jnp.arange(half, dtype=jnp.float32) * 2.0 / head_dim))
    angle = position.astype(jnp.float32)[:, None] * freq[None, :]
    cosine = jnp.cos(angle)[:, None, :]
    sine = jnp.sin(angle)[:, None, :]
    first = values[..., :half]
    second = values[..., half:]
    return jnp.concatenate(
        [first * cosine - second * sine, second * cosine + first * sine], axis=-1
    )


def attend(query, keys, values, position):
    count, heads, head_dim = query.shape
    kv_count = keys.shape[1]
    grouped = query.reshape(count, kv_count, heads // kv_count, head_dim)
    scores = (
        jnp.einsum("nkgd,mkd->kgnm", grouped, keys, preferred_element_type=jnp.float32) * attn_scale
    )
    capped = soft_cap * jnp.tanh(scores / soft_cap)
    allowed = position[None, :] <= position[:, None]
    weights = jnp.where(allowed, jnp.exp(capped), 0.0)
    probs = (weights / jnp.sum(weights, axis=-1, keepdims=True)).astype(jnp.bfloat16)
    mixed = jnp.einsum("kgnm,mkd->nkgd", probs, values, preferred_element_type=jnp.float32)
    return mixed.reshape(count, heads * head_dim).astype(jnp.bfloat16)


def swap_pairs(n_fsdp, n_tensor, turn):
    ratio = n_fsdp // n_tensor
    pairs = []
    for f in range(n_fsdp):
        for t in range(n_tensor):
            j = (f + turn) % ratio
            pairs.append((f * n_tensor + t, (t * ratio + j) * n_tensor + f // ratio))
    return pairs


def to_rows(block, n_fsdp, n_tensor):
    rows = block.shape[0]
    ratio = n_fsdp // n_tensor
    width = block.shape[1] // ratio
    f = lax.axis_index("fsdp")
    if ratio == 1:
        held = lax.ppermute(block, ("fsdp", "tensor"), swap_pairs(n_fsdp, n_tensor, 0))
    else:
        held = jnp.zeros((ratio, rows, width), block.dtype)
        for turn in range(ratio):
            piece = lax.dynamic_slice_in_dim(block, (f + turn) % ratio * width, width, 1)
            got = lax.ppermute(piece, ("fsdp", "tensor"), swap_pairs(n_fsdp, n_tensor, turn))
            held = lax.dynamic_update_index_in_dim(held, got, (f - turn) % ratio, 0)
        held = held.reshape(ratio * rows, width)
    return lax.all_gather(held, "tensor", axis=0, tiled=True)


def from_rows(summed, rows, n_fsdp, n_tensor):
    ratio = n_fsdp // n_tensor
    width = summed.shape[1]
    f = lax.axis_index("fsdp")
    back = lambda turn: [(b, a) for a, b in swap_pairs(n_fsdp, n_tensor, turn)]
    if ratio == 1:
        return lax.ppermute(summed, ("fsdp", "tensor"), back(0))
    pieces = summed.reshape(ratio, rows, width)
    out = jnp.zeros((rows, ratio * width), summed.dtype)
    for turn in range(ratio):
        piece = lax.dynamic_index_in_dim(pieces, (f - turn) % ratio, 0, keepdims=False)
        got = lax.ppermute(piece, ("fsdp", "tensor"), back(turn))
        out = lax.dynamic_update_slice_in_dim(out, got, (f + turn) % ratio * width, 1)
    return out


def solution(mesh):
    n_fsdp, n_tensor = mesh.shape["fsdp"], mesh.shape["tensor"]

    def on_device(tokens, norm_gain, w_query, w_key, w_value, w_out, post_gain):
        rows = tokens.shape[0]
        width = tokens.shape[1] * n_tensor
        widened = tokens.astype(jnp.float32)
        total = lax.psum(jnp.sum(widened * widened, axis=1), "tensor")
        normed = (
            widened * lax.rsqrt(total / width + eps_norm)[:, None] * norm_gain.astype(jnp.float32)
        ).astype(jnp.bfloat16)
        mine = to_rows(normed, n_fsdp, n_tensor)
        raw = []
        for piece in (w_query, w_key, w_value):
            part = jnp.dot(mine, piece, preferred_element_type=jnp.float32).astype(jnp.bfloat16)
            parts = lax.all_to_all(part, "fsdp", 0, 0, tiled=True)
            parts = parts.reshape(n_fsdp, rows, piece.shape[1])
            raw.append(jnp.sum(parts.astype(jnp.float32), axis=0))
        query_raw, key_raw, value_raw = raw
        position = jnp.arange(rows, dtype=jnp.int32)
        local_heads = w_query.shape[1] // HEAD_DIM
        local_kv = w_key.shape[1] // HEAD_DIM
        query = rotate(query_raw.reshape(rows, local_heads, HEAD_DIM), position)
        key = rotate(key_raw.reshape(rows, local_kv, HEAD_DIM), position)
        query, key = query.astype(jnp.bfloat16), key.astype(jnp.bfloat16)
        value = value_raw.astype(jnp.bfloat16).reshape(rows, local_kv, HEAD_DIM)
        attn = attend(query, key, value, position)
        attn_all = lax.all_gather(attn, "fsdp", axis=0, tiled=True)
        part = jnp.dot(attn_all, w_out, preferred_element_type=jnp.float32).astype(jnp.bfloat16)
        summed = lax.psum_scatter(part, "tensor", scatter_dimension=0, tiled=True)
        proj = from_rows(summed, rows, n_fsdp, n_tensor).astype(jnp.float32)
        post_total = lax.psum(jnp.sum(proj * proj, axis=1), "tensor")
        branch = (
            proj
            * lax.rsqrt(post_total / width + eps_norm)[:, None]
            * post_gain.astype(jnp.float32)
        )
        return tokens.astype(jnp.float32) + branch

    placed = (
        P(("groups", "fsdp"), "tensor"),
        P("tensor"),
        P("fsdp", "tensor"),
        P("fsdp", "tensor"),
        P("fsdp", "tensor"),
        P("tensor", "fsdp"),
        P("tensor"),
    )
    return jax.shard_map(
        on_device,
        mesh=mesh,
        in_specs=placed,
        out_specs=P(("groups", "fsdp"), "tensor"),
        check_vma=False,
    )
```

time: 605 us -> 330 us (0.55)
  waiting for transfers between devices: 542 us -> 199 us
  blocking collectives: 12 us -> 42.9 us
  starting transfers between devices: 0.19 us -> 15 us
  other arithmetic: 5.14 us -> 14.6 us
  local copies, waits for them, and re-layouts: 6.52 us -> 15.6 us
    all_gather x5 -> x2, waiting for transfers between devices: 508 us -> 97.5 us  [the longest x1 53 us: to_rows(): return lax.all_gather(held, 'tensor', axis=0, tiled=True)]
    all_to_all x0 -> x3, waiting for transfers between devices: none -> 70.5 us  [on_device(): parts = lax.all_to_all(part, 'fsdp', 0, 0, tiled=True)]
    unnamed x7 -> x3, waiting for transfers between devices: 33.7 us -> 0.05 us
    reduce_scatter x0 -> x1, waiting for transfers between devices: none -> 31.1 us  [on_device(): summed = lax.psum_scatter(part, 'tensor', scatter_dimension=0, tiled=True)]
    psum x1, blocking collectives: 5.76 us -> 34.6 us  [on_device(): post_total = lax.psum(jnp.sum(proj * proj, axis=1), 'tensor')]
    all_to_all x0 -> x3, starting transfers between devices: none -> 12.6 us  [on_device(): parts = lax.all_to_all(part, 'fsdp', 0, 0, tiled=True)]
    psum x0 -> x1, blocking collectives: none -> 8.37 us  [on_device(): total = lax.psum(jnp.sum(widened * widened, axis=1), 'tensor')]
    all_gather x1 -> x0, blocking collectives: 6.25 us -> none  [on_device(): lax.all_gather(norm_gain, 'tensor', axis=0, tiled=True)]
  transfers between devices with their start and end apart: 6 -> 8, of which waited for: 6 -> 6; matrix products, arithmetic and copies ran while one was open for 4% -> 9% of each run, Pallas kernels for 0% -> 0%
where the time goes in v1:
time: 330 us; the launch traced here: 329 us
  waiting for transfers between devices  199 us (60%)
  blocking collectives  42.9 us (13%)
  matrix products  28.5 us (9%)
  local copies, waits for them, and re-layouts  15.6 us (5%)
  starting transfers between devices  15 us (5%)
  other arithmetic  14.6 us (4%)
  between operations  13.2 us (4%)
    all_to_all x3, waiting for transfers between devices, on_device(): parts = lax.all_to_all(part, 'fsdp', 0, 0, tiled=True)  70.5 us
    all_gather x1, waiting for transfers between devices, to_rows(): return lax.all_gather(held, 'tensor', axis=0, tiled=True)  53 us
    all_gather x1, waiting for transfers between devices, on_device(): attn_all = lax.all_gather(attn, 'fsdp', axis=0, tiled=True)  44.5 us
    psum x1, blocking collectives, on_device(): post_total = lax.psum(jnp.sum(proj * proj, axis=1), 'tensor')  34.6 us
    reduce_scatter x1, waiting for transfers between devices, on_device(): summed = lax.psum_scatter(part, 'tensor', scatter_dimension=0, tiled=True)  31.1 us
    dot_general x3, matrix products, on_device(): jnp.dot(mine, piece, preferred_element_type=jnp.float32)  15.5 us
    all_to_all x3, starting transfers between devices, on_device(): parts = lax.all_to_all(part, 'fsdp', 0, 0, tiled=True)  12.6 us
    psum x1, blocking collectives, on_device(): total = lax.psum(jnp.sum(widened * widened, axis=1), 'tensor')  8.37 us
  transfers between devices with their start and end apart: 8, of which 6 were waited for; matrix products, arithmetic and copies ran while one was open for 9% of the time, Pallas kernels for 0%

profile of v1, /device:TPU:0, one launch (start us, length us, event | category | flops | bytes accessed | tf_op | source)
XLA Modules:
  0.0 329.1 jit_solution(13812048784093894810)
XLA Ops:
  6.5 1.4 fusion.2
  7.9 8.4 %psum.14 = f32[256]{0:T(256)S(1)} all-reduce(f32[256]{0:T(256)S(1)} %fusion.2), channel_id=1, replica_groups=mesh['groups'=2,'fsdp'=4,'tensor'=4] {'tensor'}, use_global_device_ids=true, to_apply=%region_1.0 | all-reduce | flops 256 | bytes 2048 | tf_op jit(solution)/shard_map/psum | solution.py:93
  16.3 0.7 convert_element_type.74
  17.0 1.3 fusion.4
  18.3 0.7 collective-permute-start
  19.0 0.8 copy-done.3
  19.8 0.0 all-gather.3.cloned.1.call-update
  19.9 53.0 %all-gather.3.cloned.1.call-done = bf16[1024,1152]{1,0:T(8,128)(2,1)} async-done(((bf16[256,1152]{1,0:T(8,128)(2,1)}), bf16[1024,1152]{1,0:T(8,128)(2,1)}) %all-gather.3.cloned.1.call-update) | async-done | bytes 2359312 | tf_op jit(solution)/shard_map/all_gather | solution.py:67
  72.9 4.5 %convolution_convert_fusion.2 = bf16[1024,512]{1,0:T(8,128)(2,1)} fusion(bf16[1024,1152]{1,0:T(8,128)(2,1)} %all-gather.3.cloned.1.call-done, bf16[1152,512]{1,0:T(8,128)(2,1)} %param.10), kind=kOutput, calls=%fused_computation.9 | convolution fusion | flops 1208483840 | bytes 4587520 | tf_op jit(solution)/shard_map/dot_general | solution.py:100
  77.3 4.6 %all-to-all-start.1 = ((bf16[4,256,512]{2,1,0:T(8,128)(2,1)}), bf16[4,256,512]{2,1,0:T(8,128)(2,1)S(1)}, u32[]{:S(2)}, u32[]{:S(2)}) async-start(bf16[4,256,512]{2,1,0:T(8,128)(2,1)} %bitcast.36), calls=%async_computation.1 | async-start | bytes 2097152 | tf_op jit(solution)/shard_map/all_to_all | solution.py:101
  81.9 4.5 %convolution_convert_fusion.3 = bf16[1024,512]{1,0:T(8,128)(2,1)} fusion(bf16[1024,1152]{1,0:T(8,128)(2,1)} %all-gather.3.cloned.1.call-done, bf16[1152,512]{1,0:T(8,128)(2,1)} %param.11), kind=kOutput, calls=%fused_computation.10 | convolution fusion | flops 1208483840 | bytes 4587520 | tf_op jit(solution)/shard_map/dot_general | solution.py:100
  86.4 21.6 %all-to-all-done.1 = bf16[4,256,512]{2,1,0:T(8,128)(2,1)S(1)} async-done(((bf16[4,256,512]{2,1,0:T(8,128)(2,1)}), bf16[4,256,512]{2,1,0:T(8,128)(2,1)S(1)}, u32[]{:S(2)}, u32[]{:S(2)}) %all-to-all-start.1) | async-done | bytes 1048608 | tf_op jit(solution)/shard_map/all_to_all | solution.py:101
  108.1 1.0 copy-done.2
  109.0 3.5 %all-to-all-start = ((bf16[4,256,512]{2,1,0:T(8,128)(2,1)}), bf16[4,256,512]{2,1,0:T(8,128)(2,1)S(1)}, u32[]{:S(2)}, u32[]{:S(2)}) async-start(bf16[4,256,512]{2,1,0:T(8,128)(2,1)} %bitcast.35), calls=%async_computation | async-start | bytes 2097152 | tf_op jit(solution)/shard_map/all_to_all | solution.py:101
  112.6 6.6 %convolution_convert_fusion.1 = bf16[1024,1024]{1,0:T(8,128)(2,1)} fusion(bf16[1024,1152]{1,0:T(8,128)(2,1)} %all-gather.3.cloned.1.call-done, bf16[1152,1024]{1,0:T(8,128)(2,1)} %param.9), kind=kOutput, calls=%fused_computation.5 | convolution fusion | flops 2416967680 | bytes 6815744 | tf_op jit(solution)/shard_map/dot_general | solution.py:100
  119.1 18.7 %all-to-all-done = bf16[4,256,512]{2,1,0:T(8,128)(2,1)S(1)} async-done(((bf16[4,256,512]{2,1,0:T(8,128)(2,1)}), bf16[4,256,512]{2,1,0:T(8,128)(2,1)S(1)}, u32[]{:S(2)}, u32[]{:S(2)}) %all-to-all-start) | async-done | bytes 1048608 | tf_op jit(solution)/shard_map/all_to_all | solution.py:101
  137.8 4.4 %all-to-all-start.2 = ((bf16[4,256,1024]{2,1,0:T(8,128)(2,1)}), bf16[4,256,1024]{2,1,0:T(8,128)(2,1)}, u32[]{:S(2)}, u32[]{:S(2)}) async-start(bf16[4,256,1024]{2,1,0:T(8,128)(2,1)} %bitcast.33), calls=%async_computation.2 | async-start | bytes 4194304 | tf_op jit(solution)/shard_map/all_to_all | solution.py:101
  142.3 0.0 all-gather.5.cloned.1.call-start
  142.3 0.3 multiply_cosine_fusion
  142.6 0.8 copy.28
  143.4 0.8 copy.30
  144.2 0.7 iota_compare_fusion
  144.8 2.2 convert_reduce_fusion.1
  147.1 2.0 copy.26
  149.1 1.9 fusion.13
  151.0 1.9 copy.41
  152.9 2.0 copy.40
  154.9 0.9 reduce_sum.58
  155.8 1.8 copy.39
  157.6 2.2 subtract_convert_fusion.1
  159.8 30.2 %all-to-all-done.2 = bf16[4,256,1024]{2,1,0:T(8,128)(2,1)} async-done(((bf16[4,256,1024]{2,1,0:T(8,128)(2,1)}), bf16[4,256,1024]{2,1,0:T(8,128)(2,1)}, u32[]{:S(2)}, u32[]{:S(2)}) %all-to-all-start.2) | async-done | bytes 2097184 | tf_op jit(solution)/shard_map/all_to_all | solution.py:101
  190.1 2.1 convert_reduce_fusion
  192.2 1.3 copy.31
  193.5 1.3 subtract_convert_fusion
  194.8 0.3 copy.32
  195.1 1.0 copy.33
  196.1 3.6 %bitcast_select_fusion = f32[4,2,256,256]{2,3,1,0:T(8,128)} fusion(pred[256,256]{0,1:T(8,128)(4,1)} %iota_compare_fusion, bf16[256,4,2,64]{3,0,2,1:T(8,128)(2,1)} %bitcast.38, bf16[256,4,2,64]{3,0,2,1:T(8,128)(2,1)S(1)} %bitcast.37, bf16[256,4,64]{2,0,1:T(8,128)(2,1)} %get-tuple-element.6, bf16[256,4,64]{2,0,1:T(8,128)(2,1)} %get-tuple-element.5), kind=kOutput, calls=%fused_computation.2 | convolution fusion | flops 137363456 | bytes 2949120 | tf_op jit(solution)/shard_map/nkgd,mkd->kgnm/dot_general | solution.py:33
  199.7 3.5 %convolution_convert_fusion.4 = bf16[4,128,2,256]{3,1,2,0:T(8,128)(2,1)} fusion(bf16[256,4,128,1]{0,2,3,1:T(8,128)(2,1)S(1)} %bitcast.40, f32[4,2,256,256]{2,3,1,0:T(8,128)} %bitcast_select_fusion), kind=kOutput, calls=%fused_computation.13 | convolution fusion | flops 135530752 | bytes 2883584 | tf_op jit(solution)/shard_map/kgnm,mkd->nkgd/dot_general | solution.py:39
  203.2 0.0 all-gather.5.cloned.1.call-update
  203.2 0.0 reduce-scatter.2.cloned.1.call-start
  203.3 44.5 %all-gather.5.cloned.1.call-done = bf16[1024,1024]{0,1:T(8,128)(2,1)} async-done(((bf16[256,1024]{0,1:T(8,128)(2,1)}), bf16[1024,1024]{0,1:T(8,128)(2,1)}) %all-gather.5.cloned.1.call-update) | async-done | bytes 2097168 | tf_op jit(solution)/shard_map/all_gather | solution.py:113
  247.8 5.9 %convolution_convert_fusion = bf16[1024,1152]{1,0:T(8,128)(2,1)} fusion(bf16[1024,1024]{0,1:T(8,128)(2,1)} %all-gather.5.cloned.1.call-done, bf16[1024,1152]{1,0:T(8,128)(2,1)S(1)} %copy-done), kind=kOutput, calls=%fused_computation.1 | convolution fusion | flops 2417098752 | bytes 6815744 | tf_op jit(solution)/shard_map/dot_general | solution.py:114
  253.7 0.0 reduce-scatter.2.cloned.1.call-update
  253.7 31.1 %reduce-scatter.2.cloned.1.call-done = bf16[256,1152]{1,0:T(8,128)(2,1)} async-done(((bf16[1024,1152]{1,0:T(8,128)(2,1)}), bf16[256,1152]{1,0:T(8,128)(2,1)}) %reduce-scatter.2.cloned.1.call-update) | async-done | bytes 589840 | tf_op jit(solution)/shard_map/reduce_scatter | solution.py:115
  284.9 1.7 collective-permute-start.1
  286.6 0.2 fusion
  286.8 34.6 %psum.15 = f32[256]{0:T(256)S(1)} all-reduce(f32[256]{0:T(256)S(1)} %fusion), channel_id=1, replica_groups=mesh['groups'=2,'fsdp'=4,'tensor'=4] {'tensor'}, use_global_device_ids=true, to_apply=%region_8.9 | all-reduce | flops 256 | bytes 2048 | tf_op jit(solution)/shard_map/psum | solution.py:117
  321.3 1.3 convert_add_fusion
  (18 shorter events, 0.1 us)
Async XLA Ops:
  6.5 241.2 %copy-start = (bf16[1024,1152]{1,0:T(8,128)(2,1)S(1)}, bf16[1024,1152]{1,0:T(8,128)(2,1)}, u32[]{:S(2)}) copy-start(bf16[1024,1152]{1,0:T(8,128)(2,1)} %param.12) | copy-start | bytes 7077892
  6.5 66.3 %all-gather.3.cloned.1.call-start = ((), (), s32[]{:S(2)}) async-start(), calls=%async_computation.4 | async-start | bytes 2949120 | tf_op jit(solution)/shard_map/all_gather | solution.py:67
  18.3 0.7 collective-permute-start
  19.0 0.8 copy-start.3
  77.3 30.7 %all-to-all-start.1 = ((bf16[4,256,512]{2,1,0:T(8,128)(2,1)}), bf16[4,256,512]{2,1,0:T(8,128)(2,1)S(1)}, u32[]{:S(2)}, u32[]{:S(2)}) async-start(bf16[4,256,512]{2,1,0:T(8,128)(2,1)} %bitcast.36), calls=%async_computation.1 | async-start | bytes 2097152 | tf_op jit(solution)/shard_map/all_to_all | solution.py:101
  108.1 1.0 copy-start.2
  109.0 28.8 %all-to-all-start = ((bf16[4,256,512]{2,1,0:T(8,128)(2,1)}), bf16[4,256,512]{2,1,0:T(8,128)(2,1)S(1)}, u32[]{:S(2)}, u32[]{:S(2)}) async-start(bf16[4,256,512]{2,1,0:T(8,128)(2,1)} %bitcast.35), calls=%async_computation | async-start | bytes 2097152 | tf_op jit(solution)/shard_map/all_to_all | solution.py:101
  137.8 52.3 %all-to-all-start.2 = ((bf16[4,256,1024]{2,1,0:T(8,128)(2,1)}), bf16[4,256,1024]{2,1,0:T(8,128)(2,1)}, u32[]{:S(2)}, u32[]{:S(2)}) async-start(bf16[4,256,1024]{2,1,0:T(8,128)(2,1)} %bitcast.33), calls=%async_computation.2 | async-start | bytes 4194304 | tf_op jit(solution)/shard_map/all_to_all | solution.py:101
  142.3 105.5 %all-gather.5.cloned.1.call-start = ((), (), s32[]{:S(2)}) async-start(), calls=%async_computation.5 | async-start | bytes 2621440 | tf_op jit(solution)/shard_map/all_gather | solution.py:113
  196.1 3.6 %copy-start.4 = (bf16[256,512]{0,1:T(8,128)(2,1)S(1)}, bf16[256,512]{0,1:T(8,128)(2,1)}, u32[]{:S(2)}) copy-start(bf16[256,512]{0,1:T(8,128)(2,1)} %copy.39) | copy-start | bytes 786436
  203.2 81.7 %reduce-scatter.2.cloned.1.call-start = ((), (), s32[]{:S(2)}) async-start(), calls=%async_computation.6 | async-start | bytes 2949120 | tf_op jit(solution)/shard_map/reduce_scatter | solution.py:115
  253.7 32.9 %copy-start.5 = (bf16[1152]{0:T(1024)(128)(2,1)S(1)}, bf16[1152]{0:T(1024)(128)(2,1)}, u32[]{:S(2)}) copy-start(bf16[1152]{0:T(1024)(128)(2,1)} %param.13) | copy-start | bytes 6916
  253.7 67.7 %copy-start.1 = (bf16[256,1152]{1,0:T(8,128)(2,1)S(1)}, bf16[256,1152]{1,0:T(8,128)(2,1)}, u32[]{:S(2)}) copy-start(bf16[256,1152]{1,0:T(8,128)(2,1)} %param.7) | copy-start | bytes 1769476
  284.9 1.7 collective-permute-start.1
Sparse Core Ops, SparseCore 0:
  20.0 52.8 all-gather.2
  203.3 44.3 all-gather.4
  253.8 30.9 reduce-scatter.1

commit v2 on v1

--- a/solution.py
+++ b/solution.py
@@ -1,6 +1,10 @@
+import functools
+
 import jax
 import jax.numpy as jnp
 from jax import lax
+from jax.experimental import pallas as pl
+from jax.experimental.pallas import tpu as pltpu
 from jax.sharding import PartitionSpec as P
 
 HEAD_DIM = 128
@@ -83,6 +87,366 @@
     return out
 
 
+MESH = pl.DeviceIdType.MESH
+VMEM_LIMIT = 60 * 1024 * 1024
+
+
+def greet(n, f, t):
+    barrier = pltpu.get_barrier_semaphore()
+
+    def signal(a, b):
+        pl.semaphore_signal(
+            barrier, inc=1, device_id={"fsdp": a, "tensor": b}, device_id_type=MESH
+        )
+
+    for k in range(1, n):
+        signal(f, lax.rem(t + k, n))
+    pl.when(f != t)(lambda: signal(t, f))
+    pl.when(f > 0)(lambda: signal(f - 1, t))
+    pl.when(f < n - 1)(lambda: signal(f + 1, t))
+    one, none = jnp.int32(1), jnp.int32(0)
+    peers = n - 1
+    for there in (f != t, f > 0, f < n - 1):
+        peers = peers + jnp.where(there, one, none)
+    pl.semaphore_wait(barrier, peers)
+
+
+def remote(src, dst, send, recv, a, b):
+    return pltpu.make_async_remote_copy(
+        src_ref=src,
+        dst_ref=dst,
+        send_sem=send,
+        recv_sem=recv,
+        device_id={"fsdp": a, "tensor": b},
+        device_id_type=MESH,
+    )
+
+
+def qkv_kernel(
+    n, cuts, x_ref, wq_ref, wk_ref, wv_ref, out_ref,
+    xs, from_low, from_high, stage,
+    local_sem, turn_send, turn_recv, cast_send, cast_recv,
+    up_send, up_recv, down_send, down_recv,
+):
+    f, t = lax.axis_index("fsdp"), lax.axis_index("tensor")
+    rows = x_ref.shape[0]
+    half = rows // cuts
+    greet(n, f, t)
+
+    def part_rows(h):
+        return pl.ds(h * half, half)
+
+    def turned(h, slot):
+        return remote(
+            x_ref.at[part_rows(h)], xs.at[slot, part_rows(h)],
+            turn_send.at[h], turn_recv.at[h], t, f,
+        )
+
+    def kept():
+        return pltpu.make_async_copy(x_ref, xs.at[t], local_sem)
+
+    def cast(h, slot, k):
+        return remote(
+            xs.at[slot, part_rows(h)], xs.at[slot, part_rows(h)],
+            cast_send.at[k - 1, h], cast_recv.at[slot, h], f, lax.rem(t + k, n),
+        )
+
+    @pl.when(f != t)
+    def _():
+        for h in range(cuts):
+            turned(h, f).start()
+
+    @pl.when(f == t)
+    def _():
+        kept().start()
+        kept().wait()
+
+    for h in range(cuts):
+        pl.when(f != t)(lambda h=h: turned(h, f).wait_recv())
+        for k in range(1, n):
+            cast(h, t, k).start()
+
+    def arrive(slot):
+        @pl.when(slot != t)
+        def _():
+            for h in range(cuts):
+                cast(h, slot, 1).wait_recv()
+
+    wide = wk_ref.shape[1]
+    count = wq_ref.shape[1] // wide + 2
+    weights = [(wq_ref, i * wide) for i in range(count - 2)] + [(wk_ref, 0), (wv_ref, 0)]
+
+    def partial(block, c):
+        ref, start = weights[c]
+        return jnp.dot(
+            xs[block], ref[:, start : start + wide], preferred_element_type=jnp.float32
+        )
+
+    def up(d, c):
+        return remote(
+            stage.at[d, c], from_low.at[d, c], up_send.at[d, c], up_recv.at[d, c], lax.rem(f + 1, n), t
+        )
+
+    def down(d, c):
+        return remote(
+            stage.at[d, c], from_high.at[d, c], down_send.at[d, c], down_recv.at[d, c], lax.rem(f + n - 1, n), t
+        )
+
+    def widened(ref, d, c):
+        return ref[d, c].astype(jnp.float32)
+
+    def travel(d, c, copy, source, first):
+        part = partial(d, c)
+
+        @pl.when(first)
+        def _():
+            stage[d, c] = part.astype(stage.dtype)
+
+        @pl.when(jnp.logical_not(first))
+        def _():
+            copy(d, c).wait_recv()
+            stage[d, c] = (part + widened(source, d, c)).astype(stage.dtype)
+
+        copy(d, c).start()
+
+    def step(s, carry):
+        high, low = n - 1 - s, s
+        pl.when(high > f)(lambda: arrive(high))
+        pl.when((low < f))(lambda: arrive(low))
+        for c in range(count):
+            pl.when(high > f)(lambda c=c: travel(high, c, up, from_low, f == 0))
+            pl.when(low < f)(lambda c=c: travel(low, c, down, from_high, f == n - 1))
+        return carry
+
+    lax.fori_loop(0, n - 1, step, 0)
+    arrive(f)
+    for c in range(count):
+        cols = slice(c * wide, (c + 1) * wide)
+        out_ref[:, cols] = partial(f, c)
+
+        @pl.when(f > 0)
+        def _():
+            up(f, c).wait_recv()
+            out_ref[:, cols] += widened(from_low, f, c)
+
+        @pl.when(f < n - 1)
+        def _():
+            down(f, c).wait_recv()
+            out_ref[:, cols] += widened(from_high, f, c)
+
+    def drain(d, carry):
+        for c in range(count):
+            pl.when(d > f)(lambda c=c: up(d, c).wait_send())
+            pl.when(d < f)(lambda c=c: down(d, c).wait_send())
+        return carry
+
+    lax.fori_loop(0, n, drain, 0)
+    for h in range(cuts):
+        pl.when(f != t)(lambda h=h: turned(h, f).wait_send())
+        for k in range(1, n):
+            cast(h, t, k).wait_send()
+
+
+def out_kernel(
+    n, cuts, kv, raw_ref, cos_ref, sin_ref, w_ref, out_ref,
+    att, stage, got, merged, landed,
+    up_send, up_recv, down_send, down_recv, plane_send, plane_recv, turn_send, turn_recv,
+):
+    f, t = lax.axis_index("fsdp"), lax.axis_index("tensor")
+    rows = raw_ref.shape[0]
+    half = rows // cuts
+    greet(n, f, t)
+    heads = w_ref.shape[0] // HEAD_DIM
+    per = heads // kv
+    wide = per * HEAD_DIM
+
+    def up(src, h):
+        return remote(
+            att.at[src, h], att.at[src, h], up_send.at[src, h], up_recv.at[src, h], lax.rem(f + 1, n), t
+        )
+
+    def down(src, h):
+        return remote(
+            att.at[src, h], att.at[src, h], down_send.at[src, h], down_recv.at[src, h], lax.rem(f + n - 1, n), t
+        )
+
+    def turn(u):
+        return (u * cos_ref[...] + pltpu.roll(u, HEAD_DIM // 2, 1) * sin_ref[...]).astype(
+            jnp.bfloat16
+        )
+
+    def piece(start):
+        return raw_ref[:, start : start + HEAD_DIM]
+
+    query_at = lax.broadcasted_iota(jnp.int32, (rows, rows), 0)
+    key_at = lax.broadcasted_iota(jnp.int32, (rows, rows), 1)
+    allowed = key_at <= query_at
+    for h in range(kv):
+        key = turn(piece((heads + h) * HEAD_DIM))
+        value = piece((heads + kv + h) * HEAD_DIM).astype(jnp.bfloat16)
+        for g in range(per):
+            query = turn(piece((h * per + g) * HEAD_DIM))
+            scores = lax.dot_general(
+                query, key, (((1,), (1,)), ((), ())), preferred_element_type=jnp.float32
+            ) * attn_scale
+            capped = soft_cap * jnp.tanh(scores / soft_cap)
+            e = jnp.where(allowed, jnp.exp(capped), 0.0)
+            probs = (e / jnp.sum(e, axis=1, keepdims=True)).astype(jnp.bfloat16)
+            mixed = jnp.dot(probs, value, preferred_element_type=jnp.float32)
+            att[f, h, :, g * HEAD_DIM : (g + 1) * HEAD_DIM] = mixed.astype(jnp.bfloat16)
+        pl.when(f < n - 1)(lambda h=h: up(f, h).start())
+        pl.when(f > 0)(lambda h=h: down(f, h).start())
+
+    def part_rows(r):
+        return pl.ds(r * half, half)
+
+    def plane(d, r, slot):
+        return remote(
+            stage.at[d, part_rows(r)], got.at[slot, part_rows(r)],
+            plane_send.at[d, r], plane_recv.at[slot, r], f, d,
+        )
+
+    def project(d):
+        for r in range(cuts):
+            span = slice(r * half, (r + 1) * half)
+            total = jnp.dot(
+                att[d, 0, span], w_ref[0:wide], preferred_element_type=jnp.float32
+            )
+            for h in range(1, kv):
+                total += jnp.dot(
+                    att[d, h, span],
+                    w_ref[h * wide : (h + 1) * wide],
+                    preferred_element_type=jnp.float32,
+                )
+            stage[d, span] = total.astype(stage.dtype)
+            pl.when(d != t)(lambda r=r: plane(d, r, t).start())
+
+    project(f)
+
+    def step(s, carry):
+        low, high = f - s, f + s
+
+        for h in range(kv):
+
+            @pl.when(low >= 0)
+            def _():
+                up(low, h).wait_recv()
+                pl.when(f < n - 1)(lambda: up(low, h).start())
+
+            @pl.when(high < n)
+            def _():
+                down(high, h).wait_recv()
+                pl.when(f > 0)(lambda: down(high, h).start())
+
+        pl.when(low >= 0)(lambda: project(low))
+        pl.when(high < n)(lambda: project(high))
+        return carry
+
+    lax.fori_loop(1, n, step, 0)
+
+    def back(r):
+        return remote(
+            merged.at[part_rows(r)], landed.at[part_rows(r)],
+            turn_send.at[r], turn_recv.at[r], t, f,
+        )
+
+    for r in range(cuts):
+        span = slice(r * half, (r + 1) * half)
+        total = stage[t, span].astype(jnp.float32)
+        for k in range(1, n):
+            slot = lax.rem(t + k, n)
+            plane(slot, r, slot).wait_recv()
+            total += got[slot, span].astype(jnp.float32)
+        merged[span] = total.astype(merged.dtype)
+        pl.when(f != t)(lambda r=r: back(r).start())
+    for r in range(cuts):
+        span = slice(r * half, (r + 1) * half)
+
+        @pl.when(f == t)
+        def _():
+            out_ref[span] = merged[span]
+
+        @pl.when(f != t)
+        def _():
+            back(r).wait_recv()
+            out_ref[span] = landed[span]
+            back(r).wait_send()
+
+    def drain(d, carry):
+        for h in range(kv):
+            pl.when((d <= f) & (f < n - 1))(lambda h=h: up(d, h).wait_send())
+            pl.when((d >= f) & (f > 0))(lambda h=h: down(d, h).wait_send())
+        for r in range(cuts):
+            pl.when(d != t)(lambda r=r: plane(d, r, t).wait_send())
+        return carry
+
+    lax.fori_loop(0, n, drain, 0)
+
+
+def in_vmem(count):
+    return [pl.BlockSpec(memory_space=pltpu.VMEM)] * count
+
+
+def project_in(n, normed, w_query, w_key, w_value):
+    rows, width = normed.shape
+    wide = w_key.shape[1]
+    count = w_query.shape[1] // wide + 2
+    cuts = 4
+    block = (n, count, rows, wide)
+    dma = pltpu.SemaphoreType.DMA
+    return pl.pallas_call(
+        functools.partial(qkv_kernel, n, cuts),
+        out_shape=jax.ShapeDtypeStruct((rows, count * wide), jnp.float32),
+        in_specs=in_vmem(4),
+        out_specs=pl.BlockSpec(memory_space=pltpu.VMEM),
+        scratch_shapes=[
+            pltpu.VMEM((n, rows, width), jnp.bfloat16),
+            pltpu.VMEM(block, jnp.bfloat16),
+            pltpu.VMEM(block, jnp.bfloat16),
+            pltpu.VMEM(block, jnp.bfloat16),
+            dma(()), dma((cuts,)), dma((cuts,)), dma((n - 1, cuts)), dma((n, cuts)),
+            dma((n, count)), dma((n, count)), dma((n, count)), dma((n, count)),
+        ],
+        compiler_params=pltpu.CompilerParams(
+            collective_id=0, has_side_effects=True, vmem_limit_bytes=VMEM_LIMIT
+        ),
+    )(normed, w_query, w_key, w_value)
+
+
+def project_out(n, raw, cosine, sine, w_out, kv):
+    rows = raw.shape[0]
+    width = w_out.shape[1]
+    cuts = 2
+    wide = w_out.shape[0] // kv
+    dma = pltpu.SemaphoreType.DMA
+    return pl.pallas_call(
+        functools.partial(out_kernel, n, cuts, kv),
+        out_shape=jax.ShapeDtypeStruct((rows, width), jnp.bfloat16),
+        in_specs=in_vmem(4),
+        out_specs=pl.BlockSpec(memory_space=pltpu.VMEM),
+        scratch_shapes=[
+            pltpu.VMEM((n, kv, rows, wide), jnp.bfloat16),
+            pltpu.VMEM((n, rows, width), jnp.bfloat16),
+            pltpu.VMEM((n, rows, width), jnp.bfloat16),
+            pltpu.VMEM((rows, width), jnp.bfloat16),
+            pltpu.VMEM((rows, width), jnp.bfloat16),
+            dma((n, kv)), dma((n, kv)), dma((n, kv)), dma((n, kv)),
+            dma((n, cuts)), dma((n, cuts)), dma((cuts,)), dma((cuts,)),
+        ],
+        compiler_params=pltpu.CompilerParams(
+            collective_id=1, has_side_effects=True, vmem_limit_bytes=VMEM_LIMIT
+        ),
+    )(raw, cosine, sine, w_out)
+
+
+def tables(rows):
+    half = HEAD_DIM // 2
+    freq = rope_base ** (-(jnp.arange(half, dtype=jnp.float32) * 2.0 / HEAD_DIM))
+    angle = jnp.arange(rows, dtype=jnp.int32).astype(jnp.float32)[:, None] * freq[None, :]
+    cosine, sine = jnp.cos(angle), jnp.sin(angle)
+    return jnp.concatenate([cosine, cosine], axis=1), jnp.concatenate([-sine, sine], axis=1)
+
+
 def solution(mesh):
     n_fsdp, n_tensor = mesh.shape["fsdp"], mesh.shape["tensor"]
 
@@ -94,26 +458,31 @@
         normed = (
             widened * lax.rsqrt(total / width + eps_norm)[:, None] * norm_gain.astype(jnp.float32)
         ).astype(jnp.bfloat16)
-        mine = to_rows(normed, n_fsdp, n_tensor)
-        raw = []
-        for piece in (w_query, w_key, w_value):
-            part = jnp.dot(mine, piece, preferred_element_type=jnp.float32).astype(jnp.bfloat16)
-            parts = lax.all_to_all(part, "fsdp", 0, 0, tiled=True)
-            parts = parts.reshape(n_fsdp, rows, piece.shape[1])
-            raw.append(jnp.sum(parts.astype(jnp.float32), axis=0))
-        query_raw, key_raw, value_raw = raw
-        position = jnp.arange(rows, dtype=jnp.int32)
-        local_heads = w_query.shape[1] // HEAD_DIM
-        local_kv = w_key.shape[1] // HEAD_DIM
-        query = rotate(query_raw.reshape(rows, local_heads, HEAD_DIM), position)
-        key = rotate(key_raw.reshape(rows, local_kv, HEAD_DIM), position)
-        query, key = query.astype(jnp.bfloat16), key.astype(jnp.bfloat16)
-        value = value_raw.astype(jnp.bfloat16).reshape(rows, local_kv, HEAD_DIM)
-        attn = attend(query, key, value, position)
-        attn_all = lax.all_gather(attn, "fsdp", axis=0, tiled=True)
-        part = jnp.dot(attn_all, w_out, preferred_element_type=jnp.float32).astype(jnp.bfloat16)
-        summed = lax.psum_scatter(part, "tensor", scatter_dimension=0, tiled=True)
-        proj = from_rows(summed, rows, n_fsdp, n_tensor).astype(jnp.float32)
+        if n_fsdp == n_tensor:
+            kv = w_key.shape[1] // HEAD_DIM
+            raw = project_in(n_fsdp, normed, w_query, w_key, w_value)
+            proj = project_out(n_fsdp, raw, *tables(rows), w_out, kv).astype(jnp.float32)
+        else:
+            mine = to_rows(normed, n_fsdp, n_tensor)
+            raw = []
+            for piece in (w_query, w_key, w_value):
+                part = jnp.dot(mine, piece, preferred_element_type=jnp.float32).astype(jnp.bfloat16)
+                parts = lax.all_to_all(part, "fsdp", 0, 0, tiled=True)
+                parts = parts.reshape(n_fsdp, rows, piece.shape[1])
+                raw.append(jnp.sum(parts.astype(jnp.float32), axis=0))
+            query_raw, key_raw, value_raw = raw
+            position = jnp.arange(rows, dtype=jnp.int32)
+            local_heads = w_query.shape[1] // HEAD_DIM
+            local_kv = w_key.shape[1] // HEAD_DIM
+            query = rotate(query_raw.reshape(rows, local_heads, HEAD_DIM), position)
+            key = rotate(key_raw.reshape(rows, local_kv, HEAD_DIM), position)
+            query, key = query.astype(jnp.bfloat16), key.astype(jnp.bfloat16)
+            value = value_raw.astype(jnp.bfloat16).reshape(rows, local_kv, HEAD_DIM)
+            attn = attend(query, key, value, position)
+            attn_all = lax.all_gather(attn, "fsdp", axis=0, tiled=True)
+            part = jnp.dot(attn_all, w_out, preferred_element_type=jnp.float32).astype(jnp.bfloat16)
+            summed = lax.psum_scatter(part, "tensor", scatter_dimension=0, tiled=True)
+            proj = from_rows(summed, rows, n_fsdp, n_tensor).astype(jnp.float32)
         post_total = lax.psum(jnp.sum(proj * proj, axis=1), "tensor")
         branch = (
             proj

time: 330 us -> 222 us (0.67)
  waiting for transfers between devices: 199 us -> 0 us
  Pallas kernels: 0 us -> 195 us
  matrix products: 28.5 us -> 0 us
  blocking collectives: 42.9 us -> 19.8 us
  local copies, waits for them, and re-layouts: 15.6 us -> 0.01 us
  starting transfers between devices: 15 us -> 0 us
  between operations: 13.2 us -> 0.04 us
  other arithmetic: 14.6 us -> 6.92 us
    pallas_call x0 -> x2, Pallas kernels: none -> 195 us  [the longest x1 108 us: project_in(): pl.pallas_call(functools.partial(qkv_kernel, n, cuts), out_shape=jax.Shap...]
    all_gather x2 -> x0, waiting for transfers between devices: 97.5 us -> none  [the longest x1 53 us: to_rows(): return lax.all_gather(held, 'tensor', axis=0, tiled=True)]
    all_to_all x3 -> x0, waiting for transfers between devices: 70.5 us -> none  [on_device(): parts = lax.all_to_all(part, 'fsdp', 0, 0, tiled=True)]
    reduce_scatter x1 -> x0, waiting for transfers between devices: 31.1 us -> none  [on_device(): summed = lax.psum_scatter(part, 'tensor', scatter_dimension=0, tiled=True)]
    dot_general x6 -> x0, matrix products: 28.5 us -> none  [the longest x3 15.5 us: on_device(): jnp.dot(mine, piece, preferred_element_type=jnp.float32)]
    psum x1, blocking collectives: 34.6 us -> 11.5 us  [on_device(): post_total = lax.psum(jnp.sum(proj * proj, axis=1), 'tensor')]
    all_to_all x3 -> x0, starting transfers between devices: 12.6 us -> none  [on_device(): parts = lax.all_to_all(part, 'fsdp', 0, 0, tiled=True)]
    unnamed x14 -> x4, local copies, waits for them, and re-layouts: 5.72 us -> 0.01 us
  transfers between devices with their start and end apart: 8 -> 0, of which waited for: 6 -> 0; matrix products, arithmetic and copies ran while one was open for 9% -> 0% of each run, Pallas kernels for 0% -> 0%
where the time goes in v2:
time: 222 us
  Pallas kernels  195 us (88%)
  blocking collectives  19.8 us (9%)
  other arithmetic  6.92 us (3%)
    pallas_call x1, Pallas kernels, project_in(): pl.pallas_call(functools.partial(qkv_kernel, n, cuts), out_shape=jax.Shap...  108 us
    pallas_call x1, Pallas kernels, project_out(): pl.pallas_call(functools.partial(out_kernel, n, cuts, kv), out_shape=jax....  86.9 us
    psum x1, blocking collectives, on_device(): post_total = lax.psum(jnp.sum(proj * proj, axis=1), 'tensor')  11.5 us
    psum x1, blocking collectives, on_device(): total = lax.psum(jnp.sum(widened * widened, axis=1), 'tensor')  8.37 us

profile of v2, /device:TPU:0, one launch (start us, length us, event | category | flops | bytes accessed | tf_op | source)
XLA Modules:
  0.0 221.6 jit_solution(15710389993457345106)
XLA Ops:
  0.0 0.0 copy-start
  0.0 0.5 fusion.5
  0.6 0.8 pad_maximum_fusion
  1.4 0.7 convert_element_type.30
  2.1 0.0 copy-done
  2.1 0.2 fusion.2
  2.3 8.4 %psum.14 = f32[256]{0:T(256)S(1)} all-reduce(f32[256]{0:T(256)S(1)} %fusion.2), channel_id=1, replica_groups=mesh['groups'=2,'fsdp'=4,'tensor'=4] {'tensor'}, use_global_device_ids=true, to_apply=%region_1.0 | all-reduce | flops 256 | bytes 2048 | tf_op jit(solution)/shard_map/psum | solution.py:457
  10.7 1.0 fusion.4.x_ref
  11.7 107.9 %shard_map.73.raw_ref = f32[256,2048]{1,0:T(8,128)} custom-call(bf16[256,1152]{1,0:T(8,128)(2,1)} %fusion.4.x_ref, bf16[1152,1024]{1,0:T(8,128)(2,1)} %wq_ref.1, bf16[1152,512]{1,0:T(8,128)(2,1)} %wk_ref.1, bf16[1152,512]{1,0:T(8,128)(2,1)} %wv_ref.1), custom_call_target="tpu_custom_call" | custom-call | tf_op jit(solution)/shard_map/pallas_call | solution.py:397
  119.6 0.0 copy-start.1
  119.6 86.9 %shard_map.74 = bf16[256,1152]{1,0:T(8,128)(2,1)} custom-call(f32[256,2048]{1,0:T(8,128)} %shard_map.73.raw_ref, f32[256,128]{1,0:T(8,128)} %get-tuple-element.8.cos_ref, f32[256,128]{1,0:T(8,128)} %get-tuple-element.9.sin_ref, bf16[1024,1152]{1,0:T(8,128)(2,1)} %w_ref.1), custom_call_target="tpu_custom_call" | custom-call | tf_op jit(solution)/shard_map/pallas_call | solution.py:422
  206.5 1.3 fusion
  207.8 11.5 %psum.15 = f32[256]{0:T(256)S(1)} all-reduce(f32[256]{0:T(256)S(1)} %fusion), channel_id=1, replica_groups=mesh['groups'=2,'fsdp'=4,'tensor'=4] {'tensor'}, use_global_device_ids=true, to_apply=%region_3.0 | all-reduce | flops 256 | bytes 2048 | tf_op jit(solution)/shard_map/psum | solution.py:486
  219.2 0.0 copy-done.1
  219.2 2.3 %convert_add_fusion = f32[256,1152]{1,0:T(8,128)} fusion(bf16[256,1152]{1,0:T(8,128)(2,1)S(1)} %copy-done, bf16[256,1152]{1,0:T(8,128)(2,1)} %shard_map.74, f32[1152]{0:T(1024)S(1)} %convert_element_type.34, f32[256]{0:T(256)S(1)} %add_rsqrt_fusion), kind=kLoop, calls=%fused_computation | loop fusion | flops 1474560 | bytes 2364928 | tf_op jit(solution)/shard_map/add | solution.py:492
  (5 shorter events, 0.0 us)
Async XLA Ops:
  0.0 2.1 copy-start
  119.6 99.7 %copy-start.1 = (bf16[1152]{0:T(1024)(128)(2,1)S(1)}, bf16[1152]{0:T(1024)(128)(2,1)}, u32[]{:S(2)}) copy-start(bf16[1152]{0:T(1024)(128)(2,1)} %param.13) | copy-start | bytes 6916

commit v3 on v2

--- a/solution.py
+++ b/solution.py
@@ -123,7 +123,7 @@
 
 
 def qkv_kernel(
-    n, cuts, x_ref, wq_ref, wk_ref, wv_ref, out_ref,
+    n, cuts, sweeps, x_ref, wq_ref, wk_ref, wv_ref, out_ref,
     xs, from_low, from_high, stage,
     local_sem, turn_send, turn_recv, cast_send, cast_recv,
     up_send, up_recv, down_send, down_recv,
@@ -134,7 +134,8 @@
     greet(n, f, t)
 
     def part_rows(h):
-        return pl.ds(h * half, half)
+        start = h * half
+        return pl.ds(start if isinstance(h, int) else pl.multiple_of(start, half), half)
 
     def turned(h, slot):
         return remote(
@@ -161,83 +162,107 @@
         kept().start()
         kept().wait()
 
-    for h in range(cuts):
-        pl.when(f != t)(lambda h=h: turned(h, f).wait_recv())
-        for k in range(1, n):
-            cast(h, t, k).start()
-
-    def arrive(slot):
+    def spread(r):
+        for i in range(cuts // sweeps):
+            h = r * (cuts // sweeps) + i
+            pl.when(f != t)(lambda h=h: turned(h, f).wait_recv())
+            for k in range(1, n):
+                cast(h, t, k).start()
+
+    spread(0)
+
+    span = rows // sweeps
+    each = cuts // sweeps
+
+    def arrive(slot, r):
         @pl.when(slot != t)
         def _():
-            for h in range(cuts):
-                cast(h, slot, 1).wait_recv()
+            for h in range(each):
+                cast(r * each + h, slot, 1).wait_recv()
+
+    def swept(r):
+        return pl.ds(pl.multiple_of(r * span, span), span)
 
     wide = wk_ref.shape[1]
     count = wq_ref.shape[1] // wide + 2
     weights = [(wq_ref, i * wide) for i in range(count - 2)] + [(wk_ref, 0), (wv_ref, 0)]
 
-    def partial(block, c):
+    def partial(block, c, r):
         ref, start = weights[c]
         return jnp.dot(
-            xs[block], ref[:, start : start + wide], preferred_element_type=jnp.float32
-        )
-
-    def up(d, c):
-        return remote(
-            stage.at[d, c], from_low.at[d, c], up_send.at[d, c], up_recv.at[d, c], lax.rem(f + 1, n), t
-        )
-
-    def down(d, c):
-        return remote(
-            stage.at[d, c], from_high.at[d, c], down_send.at[d, c], down_recv.at[d, c], lax.rem(f + n - 1, n), t
-        )
-
-    def widened(ref, d, c):
-        return ref[d, c].astype(jnp.float32)
-
-    def travel(d, c, copy, source, first):
-        part = partial(d, c)
+            xs[block, swept(r)],
+            ref[:, start : start + wide],
+            preferred_element_type=jnp.float32,
+        )
+
+    def up(d, c, r):
+        return remote(
+            stage.at[d, c, swept(r)], from_low.at[d, c, swept(r)],
+            up_send.at[d, c, r], up_recv.at[d, c, r], lax.rem(f + 1, n), t,
+        )
+
+    def down(d, c, r):
+        return remote(
+            stage.at[d, c, swept(r)], from_high.at[d, c, swept(r)],
+            down_send.at[d, c, r], down_recv.at[d, c, r], lax.rem(f + n - 1, n), t,
+        )
+
+    def widened(ref, d, c, r):
+        return ref[d, c, swept(r)].astype(jnp.float32)
+
+    def travel(d, c, r, copy, source, first):
+        part = partial(d, c, r)
 
         @pl.when(first)
         def _():
-            stage[d, c] = part.astype(stage.dtype)
+            stage[d, c, swept(r)] = part.astype(stage.dtype)
 
         @pl.when(jnp.logical_not(first))
         def _():
-            copy(d, c).wait_recv()
-            stage[d, c] = (part + widened(source, d, c)).astype(stage.dtype)
-
-        copy(d, c).start()
-
-    def step(s, carry):
-        high, low = n - 1 - s, s
-        pl.when(high > f)(lambda: arrive(high))
-        pl.when((low < f))(lambda: arrive(low))
+            copy(d, c, r).wait_recv()
+            stage[d, c, swept(r)] = (part + widened(source, d, c, r)).astype(stage.dtype)
+
+        copy(d, c, r).start()
+
+    def sweep(r, outer):
+        def step(s, carry):
+            high, low = n - 1 - s, s
+            pl.when(high > f)(lambda: arrive(high, r))
+            pl.when(low < f)(lambda: arrive(low, r))
+            for c in range(count):
+                pl.when(high > f)(lambda c=c: travel(high, c, r, up, from_low, f == 0))
+                pl.when(low < f)(lambda c=c: travel(low, c, r, down, from_high, f == n - 1))
+            pl.when((s == 0) & (r + 1 < sweeps))(lambda: spread(r + 1))
+            return carry
+
+        return lax.fori_loop(0, n - 1, step, outer)
+
+    def finish(r, carry):
+        arrive(f, r)
         for c in range(count):
-            pl.when(high > f)(lambda c=c: travel(high, c, up, from_low, f == 0))
-            pl.when(low < f)(lambda c=c: travel(low, c, down, from_high, f == n - 1))
+            cols = slice(c * wide, (c + 1) * wide)
+            out_ref[swept(r), cols] = partial(f, c, r)
+
+            @pl.when(f > 0)
+            def _():
+                up(f, c, r).wait_recv()
+                out_ref[swept(r), cols] += widened(from_low, f, c, r)
+
+            @pl.when(f < n - 1)
+            def _():
+                down(f, c, r).wait_recv()
+                out_ref[swept(r), cols] += widened(from_high, f, c, r)
+
         return carry
 
-    lax.fori_loop(0, n - 1, step, 0)
-    arrive(f)
-    for c in range(count):
-        cols = slice(c * wide, (c + 1) * wide)
-        out_ref[:, cols] = partial(f, c)
-
-        @pl.when(f > 0)
-        def _():
-            up(f, c).wait_recv()
-            out_ref[:, cols] += widened(from_low, f, c)
-
-        @pl.when(f < n - 1)
-        def _():
-            down(f, c).wait_recv()
-            out_ref[:, cols] += widened(from_high, f, c)
+    lax.fori_loop(0, sweeps, sweep, 0)
+    lax.fori_loop(0, sweeps, finish, 0)
 
     def drain(d, carry):
         for c in range(count):
-            pl.when(d > f)(lambda c=c: up(d, c).wait_send())
-            pl.when(d < f)(lambda c=c: down(d, c).wait_send())
+            for r in range(sweeps):
+                pl.when(d > f)(lambda c=c, r=r: up(d, c, r).wait_send())
+                pl.when(d < f)(lambda c=c, r=r: down(d, c, r).wait_send())
         return carry
 
     lax.fori_loop(0, n, drain, 0)
@@ -258,47 +283,52 @@
     greet(n, f, t)
     heads = w_ref.shape[0] // HEAD_DIM
     per = heads // kv
-    wide = per * HEAD_DIM
-
-    def up(src, h):
-        return remote(
-            att.at[src, h], att.at[src, h], up_send.at[src, h], up_recv.at[src, h], lax.rem(f + 1, n), t
-        )
-
-    def down(src, h):
-        return remote(
-            att.at[src, h], att.at[src, h], down_send.at[src, h], down_recv.at[src, h], lax.rem(f + n - 1, n), t
-        )
+
+    def part_rows(r):
+        return pl.ds(r * half, half)
+
+    def up(src, r):
+        return remote(
+            att.at[src, part_rows(r)], att.at[src, part_rows(r)],
+            up_send.at[src, r], up_recv.at[src, r], lax.rem(f + 1, n), t,
+        )
+
+    def down(src, r):
+        return remote(
+            att.at[src, part_rows(r)], att.at[src, part_rows(r)],
+            down_send.at[src, r], down_recv.at[src, r], lax.rem(f + n - 1, n), t,
+        )
+
+    def turn_rows(u, span):
+        other = pltpu.roll(u, HEAD_DIM // 2, 1)
+        return (u * cos_ref[span] + other * sin_ref[span]).astype(jnp.bfloat16)
 
     def turn(u):
-        return (u * cos_ref[...] + pltpu.roll(u, HEAD_DIM // 2, 1) * sin_ref[...]).astype(
-            jnp.bfloat16
-        )
+        return turn_rows(u, slice(0, rows))
 
     def piece(start):
         return raw_ref[:, start : start + HEAD_DIM]
 
-    query_at = lax.broadcasted_iota(jnp.int32, (rows, rows), 0)
-    key_at = lax.broadcasted_iota(jnp.int32, (rows, rows), 1)
-    allowed = key_at <= query_at
-    for h in range(kv):
-        key = turn(piece((heads + h) * HEAD_DIM))
-        value = piece((heads + kv + h) * HEAD_DIM).astype(jnp.bfloat16)
-        for g in range(per):
-            query = turn(piece((h * per + g) * HEAD_DIM))
+    keys = [turn(piece((heads + h) * HEAD_DIM)) for h in range(kv)]
+    values = [piece((heads + kv + h) * HEAD_DIM).astype(jnp.bfloat16) for h in range(kv)]
+    for r in range(cuts):
+        span, seen = slice(r * half, (r + 1) * half), (r + 1) * half
+        query_at = r * half + lax.broadcasted_iota(jnp.int32, (half, seen), 0)
+        allowed = lax.broadcasted_iota(jnp.int32, (half, seen), 1) <= query_at
+        for g in range(heads):
+            h = g // per
+            query = turn_rows(piece(g * HEAD_DIM)[span], span)
             scores = lax.dot_general(
-                query, key, (((1,), (1,)), ((), ())), preferred_element_type=jnp.float32
+                query, keys[h][:seen], (((1,), (1,)), ((), ())),
+                preferred_element_type=jnp.float32,
             ) * attn_scale
             capped = soft_cap * jnp.tanh(scores / soft_cap)
             e = jnp.where(allowed, jnp.exp(capped), 0.0)
             probs = (e / jnp.sum(e, axis=1, keepdims=True)).astype(jnp.bfloat16)
-            mixed = jnp.dot(probs, value, preferred_element_type=jnp.float32)
-            att[f, h, :, g * HEAD_DIM : (g + 1) * HEAD_DIM] = mixed.astype(jnp.bfloat16)
-        pl.when(f < n - 1)(lambda h=h: up(f, h).start())
-        pl.when(f > 0)(lambda h=h: down(f, h).start())
-
-    def part_rows(r):
-        return pl.ds(r * half, half)
+            mixed = jnp.dot(probs, values[h][:seen], preferred_element_type=jnp.float32)
+            att[f, span, g * HEAD_DIM : (g + 1) * HEAD_DIM] = mixed.astype(jnp.bfloat16)
+        pl.when(f < n - 1)(lambda r=r: up(f, r).start())
+        pl.when(f > 0)(lambda r=r: down(f, r).start())
 
     def plane(d, r, slot):
         return remote(
@@ -306,43 +336,27 @@
             plane_send.at[d, r], plane_recv.at[slot, r], f, d,
         )
 
-    def project(d):
-        for r in range(cuts):
-            span = slice(r * half, (r + 1) * half)
-            total = jnp.dot(
-                att[d, 0, span], w_ref[0:wide], preferred_element_type=jnp.float32
-            )
-            for h in range(1, kv):
-                total += jnp.dot(
-                    att[d, h, span],
-                    w_ref[h * wide : (h + 1) * wide],
-                    preferred_element_type=jnp.float32,
-                )
-            stage[d, span] = total.astype(stage.dtype)
-            pl.when(d != t)(lambda r=r: plane(d, r, t).start())
-
-    project(f)
-
-    def step(s, carry):
+    def project(d, r):
+        span = slice(r * half, (r + 1) * half)
+        total = jnp.dot(att[d, span], w_ref[...], preferred_element_type=jnp.float32)
+        stage[d, span] = total.astype(stage.dtype)
+        pl.when(d != t)(lambda: plane(d, r, t).start())
+
+    def step(s, r):
         low, high = f - s, f + s
 
-        for h in range(kv):
-
-            @pl.when(low >= 0)
-            def _():
-                up(low, h).wait_recv()
-                pl.when(f < n - 1)(lambda: up(low, h).start())
-
-            @pl.when(high < n)
-            def _():
-                down(high, h).wait_recv()
-                pl.when(f > 0)(lambda: down(high, h).start())
-
-        pl.when(low >= 0)(lambda: project(low))
-        pl.when(high < n)(lambda: project(high))
-        return carry
-
-    lax.fori_loop(1, n, step, 0)
+        @pl.when(low >= 0)
+        def _():
+            up(low, r).wait_recv()
+            pl.when(f < n - 1)(lambda: up(low, r).start())
+
+        @pl.when(high < n)
+        def _():
+            down(high, r).wait_recv()
+            pl.when(f > 0)(lambda: down(high, r).start())
+
+        pl.when(low >= 0)(lambda: project(low, r))
+        pl.when(high < n)(lambda: project(high, r))
 
     def back(r):
         return remote(
@@ -350,7 +364,7 @@
             turn_send.at[r], turn_recv.at[r], t, f,
         )
 
-    for r in range(cuts):
+    def merge(r):
         span = slice(r * half, (r + 1) * half)
         total = stage[t, span].astype(jnp.float32)
         for k in range(1, n):
@@ -358,7 +372,15 @@
             plane(slot, r, slot).wait_recv()
             total += got[slot, span].astype(jnp.float32)
         merged[span] = total.astype(merged.dtype)
-        pl.when(f != t)(lambda r=r: back(r).start())
+        pl.when(f != t)(lambda: back(r).start())
+
+    for r in range(cuts):
+        project(f, r)
+        for s in range(1, n):
+            step(s, r)
+            if s == 1 and r > 0:
+                merge(r - 1)
+    merge(cuts - 1)
     for r in range(cuts):
         span = slice(r * half, (r + 1) * half)
 
@@ -373,10 +395,9 @@
             back(r).wait_send()
 
     def drain(d, carry):
-        for h in range(kv):
-            pl.when((d <= f) & (f < n - 1))(lambda h=h: up(d, h).wait_send())
-            pl.when((d >= f) & (f > 0))(lambda h=h: down(d, h).wait_send())
         for r in range(cuts):
+            pl.when((d <= f) & (f < n - 1))(lambda r=r: up(d, r).wait_send())
+            pl.when((d >= f) & (f > 0))(lambda r=r: down(d, r).wait_send())
             pl.when(d != t)(lambda r=r: plane(d, r, t).wait_send())
         return carry
 
@@ -391,11 +412,11 @@
     rows, width = normed.shape
     wide = w_key.shape[1]
     count = w_query.shape[1] // wide + 2
-    cuts = 4
+    cuts, sweeps = 4, 2
     block = (n, count, rows, wide)
     dma = pltpu.SemaphoreType.DMA
     return pl.pallas_call(
-        functools.partial(qkv_kernel, n, cuts),
+        functools.partial(qkv_kernel, n, cuts, sweeps),
         out_shape=jax.ShapeDtypeStruct((rows, count * wide), jnp.float32),
         in_specs=in_vmem(4),
         out_specs=pl.BlockSpec(memory_space=pltpu.VMEM),
@@ -405,7 +426,7 @@
             pltpu.VMEM(block, jnp.bfloat16),
             pltpu.VMEM(block, jnp.bfloat16),
             dma(()), dma((cuts,)), dma((cuts,)), dma((n - 1, cuts)), dma((n, cuts)),
-            dma((n, count)), dma((n, count)), dma((n, count)), dma((n, count)),
+            *[dma((n, count, sweeps))] * 4,
         ],
         compiler_params=pltpu.CompilerParams(
             collective_id=0, has_side_effects=True, vmem_limit_bytes=VMEM_LIMIT
@@ -417,7 +438,6 @@
     rows = raw.shape[0]
     width = w_out.shape[1]
     cuts = 2
-    wide = w_out.shape[0] // kv
     dma = pltpu.SemaphoreType.DMA
     return pl.pallas_call(
         functools.partial(out_kernel, n, cuts, kv),
@@ -425,12 +445,12 @@
         in_specs=in_vmem(4),
         out_specs=pl.BlockSpec(memory_space=pltpu.VMEM),
         scratch_shapes=[
-            pltpu.VMEM((n, kv, rows, wide), jnp.bfloat16),
+            pltpu.VMEM((n, rows, w_out.shape[0]), jnp.bfloat16),
             pltpu.VMEM((n, rows, width), jnp.bfloat16),
             pltpu.VMEM((n, rows, width), jnp.bfloat16),
             pltpu.VMEM((rows, width), jnp.bfloat16),
             pltpu.VMEM((rows, width), jnp.bfloat16),
-            dma((n, kv)), dma((n, kv)), dma((n, kv)), dma((n, kv)),
+            *[dma((n, cuts))] * 4,
             dma((n, cuts)), dma((n, cuts)), dma((cuts,)), dma((cuts,)),
         ],
         compiler_params=pltpu.CompilerParams(

time: 222 us -> 216 us (0.973)
  Pallas kernels: 195 us -> 189 us
    pallas_call x1, Pallas kernels: 86.9 us -> 70.8 us  [project_out(): pl.pallas_call(functools.partial(out_kernel, n, cuts, kv), out_shape=jax....]
    pallas_call x1, Pallas kernels: 108 us -> 118 us  [project_in(): pl.pallas_call(functools.partial(qkv_kernel, n, cuts, sweeps), out_shape=...]
where the time goes in v3:
time: 216 us
  Pallas kernels  189 us (88%)
  blocking collectives  19.9 us (9%)
  other arithmetic  6.92 us (3%)
    pallas_call x1, Pallas kernels, project_in(): pl.pallas_call(functools.partial(qkv_kernel, n, cuts, sweeps), out_shape=...  118 us
    pallas_call x1, Pallas kernels, project_out(): pl.pallas_call(functools.partial(out_kernel, n, cuts, kv), out_shape=jax....  70.8 us
    psum x1, blocking collectives, on_device(): post_total = lax.psum(jnp.sum(proj * proj, axis=1), 'tensor')  11.5 us
    psum x1, blocking collectives, on_device(): total = lax.psum(jnp.sum(widened * widened, axis=1), 'tensor')  8.37 us

profile of v3, /device:TPU:0, one launch (start us, length us, event | category | flops | bytes accessed | tf_op | source)
XLA Modules:
  0.0 215.5 jit_solution(8263771215529955943)
XLA Ops:
  0.0 0.0 copy-start
  0.0 0.5 fusion.5
  0.6 0.8 pad_maximum_fusion
  1.4 0.7 convert_element_type.30
  2.1 0.0 copy-done
  2.1 0.2 fusion.2
  2.3 8.4 %psum.14 = f32[256]{0:T(256)S(1)} all-reduce(f32[256]{0:T(256)S(1)} %fusion.2), channel_id=1, replica_groups=mesh['groups'=2,'fsdp'=4,'tensor'=4] {'tensor'}, use_global_device_ids=true, to_apply=%region_1.0 | all-reduce | flops 256 | bytes 2048 | tf_op jit(solution)/shard_map/psum | solution.py:477
  10.7 1.0 fusion.4.x_ref
  11.7 117.8 %shard_map.73.raw_ref = f32[256,2048]{1,0:T(8,128)} custom-call(bf16[256,1152]{1,0:T(8,128)(2,1)} %fusion.4.x_ref, bf16[1152,1024]{1,0:T(8,128)(2,1)} %wq_ref.1, bf16[1152,512]{1,0:T(8,128)(2,1)} %wk_ref.1, bf16[1152,512]{1,0:T(8,128)(2,1)} %wv_ref.1), custom_call_target="tpu_custom_call" | custom-call | tf_op jit(solution)/shard_map/pallas_call | solution.py:418
  129.5 0.0 copy-start.1
  129.5 70.8 %shard_map.74 = bf16[256,1152]{1,0:T(8,128)(2,1)} custom-call(f32[256,2048]{1,0:T(8,128)} %shard_map.73.raw_ref, f32[256,128]{1,0:T(8,128)} %get-tuple-element.8.cos_ref, f32[256,128]{1,0:T(8,128)} %get-tuple-element.9.sin_ref, bf16[1024,1152]{1,0:T(8,128)(2,1)} %w_ref.1), custom_call_target="tpu_custom_call" | custom-call | tf_op jit(solution)/shard_map/pallas_call | solution.py:442
  200.4 1.3 fusion
  201.7 11.5 %psum.15 = f32[256]{0:T(256)S(1)} all-reduce(f32[256]{0:T(256)S(1)} %fusion), channel_id=1, replica_groups=mesh['groups'=2,'fsdp'=4,'tensor'=4] {'tensor'}, use_global_device_ids=true, to_apply=%region_3.0 | all-reduce | flops 256 | bytes 2048 | tf_op jit(solution)/shard_map/psum | solution.py:506
  213.2 0.0 copy-done.1
  213.2 2.3 %convert_add_fusion = f32[256,1152]{1,0:T(8,128)} fusion(bf16[256,1152]{1,0:T(8,128)(2,1)S(1)} %copy-done, bf16[256,1152]{1,0:T(8,128)(2,1)} %shard_map.74, f32[1152]{0:T(1024)S(1)} %convert_element_type.34, f32[256]{0:T(256)S(1)} %add_rsqrt_fusion), kind=kLoop, calls=%fused_computation | loop fusion | flops 1474560 | bytes 2364928 | tf_op jit(solution)/shard_map/add | solution.py:512
  (5 shorter events, 0.0 us)
Async XLA Ops:
  0.0 2.1 copy-start
  129.5 83.6 %copy-start.1 = (bf16[1152]{0:T(1024)(128)(2,1)S(1)}, bf16[1152]{0:T(1024)(128)(2,1)}, u32[]{:S(2)}) copy-start(bf16[1152]{0:T(1024)(128)(2,1)} %param.13) | copy-start | bytes 6916
